TPU v7x, 32 devices: a whole 2x2x4 slice. The times are simulated.
32 devices in a mesh: section: 4 (over z), dp: 2 (over y), tensor: 4 (over x, core).
Axes of the slice: x: 2, y: 2, z: 4, core: 2. Of those that a mesh axis runs over, the one named last changes fastest.
Arguments:
- inputs: bfloat16 [8, 2, 64, 2560], P('dp', None, None, ('section', 'tensor')), parts along dimension 0, may hold values from -18 to 18
- sequence_jobs: int32 [8, 2, 1], P('dp'), parts along dimension 0, may hold values from 0 to 3
- entry_sequence: int32 [8], P('dp'), parts along dimension 0, may hold values from 0 to 3, each once
- layer_norm_gain: float32 [4, 2560], P('section'), may hold values from 0.25 to 1.75
- frozen_query_matrix: bfloat16 [4, 2560, 2560], P('section', None, 'tensor'), may hold values from -1 to 1
- frozen_key_matrix: bfloat16 [4, 2560, 2560], P('section', None, 'tensor'), may hold values from -24 to 24
- frozen_value_matrix: bfloat16 [4, 2560, 2560], P('section', None, 'tensor'), may hold values from -0.125 to 0.125
- frozen_output_matrix: bfloat16 [4, 2560, 2560], P('section', 'tensor'), may hold values from -0.125 to 0.125
- adapter_down_maps: bfloat16 [4, 2560, 128], P('section', 'tensor'), may hold values from -0.125 to 0.125
- adapter_up_maps: bfloat16 [4, 2, 64, 2560], P('section', None, None, 'tensor'), may hold values from -1.5 to 1.5
Outputs:
- finished: bfloat16 [8, 2, 64, 2560], P('dp', None, None, ('section', 'tensor')), parts along dimension 0
There are 2 independent parts, one for each index of `dp`. A program takes and returns all parts, laid end to end along the dimension named above; an argument that names none is the same for every part. Nothing has to cross between parts.
Inputs may be any that keep to these rules, and one draw needn't show every extreme that they name: `sequence_jobs`: every one of the 4 jobs owns at least one sequence. `entry_sequence`: a permutation of the 4 micro-batches.
All inputs are finite; a program needn't handle non-finite values.
Results may differ from a plain program's by a relative error of at most 0.039.
Values may be sent and summed in bfloat16 or wider, within the bound.
A program may use at most 64 MiB of HBM per device.

v0:
```python
import jax
import jax.numpy as jnp
from jax import lax
from jax.sharding import PartitionSpec as P

HEAD_DIM = 128
ADAPTER_RANK = 16
ADAPTER_JOBS = 4
adapter_scale = 2.0


def shifted(value, axis, steps):
    count = lax.axis_size(axis)
    leading, last = (max(0, -steps), min(count, count - steps))
    return lax.ppermute(value, axis, [(source, source + steps) for source in range(leading, last)])


def spread(array, axis, root):
    mine = lax.axis_index(axis) == root
    return lax.psum(jnp.where(mine, array, jnp.zeros_like(array)), axis)


def attend(query_rows, key_vecs, value_rows, head_groupings, sequence_length):
    head_count = query_rows.shape[1] // HEAD_DIM
    grid_shape = (head_groupings, sequence_length, head_count, HEAD_DIM)
    scores = jnp.einsum(
        "bqhd,bkhd->bhqk",
        query_rows.reshape(grid_shape),
        key_vecs.reshape(grid_shape),
        preferred_element_type=jnp.float32,
    ) * HEAD_DIM ** (-0.5)
    causal = lax.broadcasted_iota(
        jnp.int32, (sequence_length, sequence_length), 0
    ) >= lax.broadcasted_iota(jnp.int32, (sequence_length, sequence_length), 1)
    scores = jnp.where(causal, scores, -jnp.inf)
    row_max = jnp.max(scores, axis=-1, keepdims=True)
    weights = jnp.exp(scores - row_max)
    probabilities = (weights / jnp.sum(weights, axis=-1, keepdims=True)).astype(jnp.bfloat16)
    mixture = jnp.einsum(
        "bhqk,bkhd->bqhd",
        probabilities,
        value_rows.reshape(grid_shape),
        preferred_element_type=jnp.float32,
    )
    return mixture.astype(jnp.bfloat16).reshape(
        head_groupings * sequence_length, head_count * HEAD_DIM
    )


def prepare_inputs(
    complete_result, inverse_norm_scale, adapter_rows, partition_number, column_slice
):
    widened = complete_result.astype(jnp.float32)
    meansq = jnp.mean(widened * widened, axis=-1, keepdims=True)
    normalized_input = (widened * lax.rsqrt(meansq + 1e-05) * inverse_norm_scale).astype(
        jnp.bfloat16
    )
    local_normalized = lax.dynamic_slice_in_dim(
        normalized_input, partition_number * column_slice, column_slice, 1
    )
    return (
        normalized_input,
        jnp.dot(local_normalized, adapter_rows, preferred_element_type=jnp.float32),
    )


def final_output(
    normalized_input,
    lowrank_products,
    query_matrix,
    key_matrix,
    value_matrix,
    output_matrix,
    adapter_upper_part,
    head_groupings,
    sequence_length,
):
    middle_result = lowrank_products.shape[1] // 2
    query_rows = (
        jnp.dot(normalized_input, query_matrix, preferred_element_type=jnp.float32)
        + adapter_scale
        * jnp.dot(
            lowrank_products[:, :middle_result],
            adapter_upper_part[0],
            preferred_element_type=jnp.float32,
        )
    ).astype(jnp.bfloat16)
    key_vecs = jnp.dot(normalized_input, key_matrix, preferred_element_type=jnp.float32).astype(
        jnp.bfloat16
    )
    value_rows = (
        jnp.dot(normalized_input, value_matrix, preferred_element_type=jnp.float32)
        + adapter_scale
        * jnp.dot(
            lowrank_products[:, middle_result:],
            adapter_upper_part[1],
            preferred_element_type=jnp.float32,
        )
    ).astype(jnp.bfloat16)
    heads = attend(query_rows, key_vecs, value_rows, head_groupings, sequence_length)
    return (
        jnp.dot(heads, output_matrix, preferred_element_type=jnp.float32)
        .astype(jnp.bfloat16)
        .astype(jnp.float32)
    )


def shards(
    inputs,
    sequence_jobs,
    entry_sequence,
    layer_norm_gain,
    frozen_query_matrix,
    frozen_key_matrix,
    frozen_value_matrix,
    frozen_output_matrix,
    adapter_down_maps,
    adapter_up_maps,
):
    sections = lax.axis_size("section")
    across = lax.axis_size("tensor")
    section_id = lax.axis_index("section")
    partition_number = lax.axis_index("tensor")
    entire = lax.all_gather(inputs, ("section", "tensor"), axis=3, tiled=True)
    batches, head_groupings, sequence_length, features = entire.shape
    column_slice = frozen_query_matrix.shape[2]
    lowrank_width = adapter_down_maps.shape[2]
    tok_rows = head_groupings * sequence_length
    step_count = batches + sections - 1

    def compute(complete_result, step_idx):
        position = step_idx - section_id
        active = jnp.logical_and(position >= 0, position < batches)
        chosen = entry_sequence[jnp.clip(position, 0, batches - 1)]
        seq_jobs = lax.dynamic_index_in_dim(sequence_jobs, chosen, 0, keepdims=False)
        job_per_row = jnp.repeat(seq_jobs[:, 0], sequence_length)
        normalized_input, part_codes = lax.cond(
            active,
            lambda: prepare_inputs(
                complete_result,
                layer_norm_gain[0],
                adapter_down_maps[0],
                partition_number,
                column_slice,
            ),
            lambda: (
                jnp.zeros((tok_rows, features), jnp.bfloat16),
                jnp.zeros((tok_rows, lowrank_width), jnp.float32),
            ),
        )
        summed_codes = lax.psum(part_codes, "tensor")
        column_job = (
            lax.broadcasted_iota(jnp.int32, (lowrank_width,), 0) // ADAPTER_RANK % ADAPTER_JOBS
        )
        lowrank_products = jnp.where(
            column_job[None, :] == job_per_row[:, None], summed_codes, 0.0
        ).astype(jnp.bfloat16)
        return lax.cond(
            active,
            lambda: final_output(
                normalized_input,
                lowrank_products,
                frozen_query_matrix[0],
                frozen_key_matrix[0],
                frozen_value_matrix[0],
                frozen_output_matrix[0],
                adapter_up_maps[0],
                head_groupings,
                sequence_length,
            ),
            lambda: jnp.zeros((tok_rows, features), jnp.float32),
        )

    def injected(step_idx):
        chosen = entry_sequence[jnp.minimum(step_idx, batches - 1)]
        return lax.dynamic_index_in_dim(entire, chosen, 0, keepdims=False).reshape(
            tok_rows, features
        )

    def record(stored, step_idx, piece):
        out_slot = step_idx - (sections - 1)
        keeping = jnp.logical_and(section_id == sections - 1, out_slot >= 0)
        updated = lax.dynamic_update_index_in_dim(stored, piece, jnp.maximum(out_slot, 0), 0)
        return jnp.where(keeping, updated, stored)

    stored = jnp.zeros((batches, tok_rows, column_slice), jnp.bfloat16)

    def advance(step_idx, carried):
        arrived, stored = carried
        entering = lax.dynamic_slice_in_dim(
            injected(step_idx), partition_number * column_slice, column_slice, 1
        )
        owned = jnp.where(section_id == 0, entering, arrived)
        complete_result = lax.all_gather(owned, "tensor", axis=1, tiled=True)
        term = compute(complete_result, step_idx)
        share = lax.psum_scatter(
            term.astype(jnp.bfloat16), "tensor", scatter_dimension=1, tiled=True
        ).astype(jnp.float32)
        updated_x = (owned.astype(jnp.float32) + share).astype(jnp.bfloat16)
        stored = record(stored, step_idx, updated_x)
        arrived = shifted(updated_x, ("section", "tensor"), across)
        return (arrived, stored)

    initial = jnp.zeros((tok_rows, column_slice), jnp.bfloat16)
    arrived, stored = lax.fori_loop(0, step_count, advance, (initial, stored))
    result = spread(stored, "section", sections - 1)
    complete = lax.all_gather(result, "tensor", axis=2, tiled=True)
    width = features // (sections * across)
    piece = lax.dynamic_slice_in_dim(
        complete, (section_id * across + partition_number) * width, width, 2
    )
    return piece.reshape(batches, head_groupings, sequence_length, width)


def solution(mesh):
    in_specs = (
        P("dp", None, None, ("section", "tensor")),
        P("dp", None, None),
        P("dp"),
        P("section", None),
        P("section", None, "tensor"),
        P("section", None, "tensor"),
        P("section", None, "tensor"),
        P("section", "tensor", None),
        P("section", "tensor", None),
        P("section", None, None, "tensor"),
    )
    out_specs = P("dp", None, None, ("section", "tensor"))
    return jax.shard_map(shards, mesh=mesh, in_specs=in_specs, out_specs=out_specs, check_vma=False)
```

profile of v0, /device:TPU:0, one launch (start us, length us, event | category | flops | bytes accessed | tf_op | source)
XLA Modules:
  0.0 737.4 jit_solution(598932090509238109)
XLA Ops:
  9.2 58.9 %all-gather.3.cloned.1.call-done = bf16[4,2,64,2560]{2,0,1,3:T(4,128)(2,1)} async-done(((bf16[4,2,64,160]{2,0,1,3:T(4,128)(2,1)}), bf16[4,2,64,2560]{2,0,1,3:T(4,128)(2,1)}) %all-gather.3.cloned.1.call-update) | async-done | bytes 2621456 | tf_op jit(solution)/shard_map/all_gather | solution.py:124
  68.1 8.5 %copy.28 = bf16[4,2,64,2560]{3,2,1,0:T(8,128)(2,1)} copy(bf16[4,2,64,2560]{2,0,1,3:T(4,128)(2,1)} %all-gather.3.cloned.1.call-done) | data formatting | bytes 5242880 | tf_op jit(solution)/shard_map/while | solution.py:205
  77.5 579.8 %while.17 = (s32[]{:T(128)}, bf16[128,640]{1,0:T(8,128)(2,1)S(1)}, bf16[4,128,640]{2,1,0:T(8,128)(2,1)}, pred[]{:T(512)}, s32[4]{0:T(128)S(1)}, /*index=5*/bf16[...) while((s32[]{:T(128)}, bf16[128,640]{1,0:T(8,128)(2,1)S(1)}, ...), condition=%wide.region_10.11_spmd, body=%wide.region_0.10_spmd.sunk | while | flops 1744747648 | bytes 44909328 | solution.py:205
  82.6 7.9 %all_gather.19 = bf16[128,2560]{1,0:T(8,128)(2,1)S(1)} all-gather(bf16[128,640]{1,0:T(8,128)(2,1)S(1)} %dynamic-slice_select_fusion.2), channel_id=1, replica_groups=mesh['section'=4,'dp'=2,'tensor'=4] {'tensor'}, dimensions={1}, use_global_device_ids=true | all-gather | bytes 819200 | tf_op jit(solution)/shard_map/while/body/eval_jaxpr/all_gather | solution.py:194
  93.0 11.1 %psum.23 = bf16[128,128]{1,0:T(8,128)(2,1)S(1)} all-reduce(f32[128,128]{1,0:T(8,128)S(1)} %get-tuple-element.638), channel_id=1, replica_groups=mesh['section'=4,'dp'=2,'tensor'=4] {'tensor'}, use_global_device_ids=true, to_apply=%region_4.4 | all-reduce | flops 16384 | bytes 98304 | tf_op jit(solution)/shard_map/while/body/eval_jaxpr/psum | solution.py:151
  105.1 22.0 %conditional.5 = (bf16[128,2560]{1,0:T(8,128)(2,1)S(1)}) conditional(s32[]{:T(128)} %convert_element_type.120, () %tuple.63, (bf16[1,2560,640]{2,1,0:T(8,128)(2,1)}, bf16[128,2560]{1,0:T(8,128)(2,1)}, bf16[128,128]{1,0:T(8,128)(2,1)S(1)}, bf16[1,2,64,640]{3,2,1,0:T(8,128)(2,1)}, bf16[1,2560,640]{2,1,0:T(8,128)(2,1)}, ...), branch_computations={%region_5.5_spmd, %region_6.8_spmd} | conditional | flops 1720939136 | bytes 34157632 | solution.py:158
  128.3 20.7 %reduce-scatter.6.cloned.1.call-done = bf16[640,128]{1,0:T(8,128)(2,1)} async-done(((bf16[2560,128]{1,0:T(8,128)(2,1)}), bf16[640,128]{1,0:T(8,128)(2,1)}) %reduce-scatter.6.cloned.1.call-update) | async-done | bytes 163856 | tf_op jit(solution)/shard_map/while
  172.9 12.0 %psum.23 = bf16[128,128]{1,0:T(8,128)(2,1)S(1)} all-reduce(f32[128,128]{1,0:T(8,128)S(1)} %get-tuple-element.638), channel_id=1, replica_groups=mesh['section'=4,'dp'=2,'tensor'=4] {'tensor'}, use_global_device_ids=true, to_apply=%region_4.4 | all-reduce | flops 16384 | bytes 98304 | tf_op jit(solution)/shard_map/while/body/eval_jaxpr/psum | solution.py:151
  185.8 22.1 %conditional.5 = (bf16[128,2560]{1,0:T(8,128)(2,1)S(1)}) conditional(s32[]{:T(128)} %convert_element_type.120, () %tuple.63, (bf16[1,2560,640]{2,1,0:T(8,128)(2,1)}, bf16[128,2560]{1,0:T(8,128)(2,1)}, bf16[128,128]{1,0:T(8,128)(2,1)S(1)}, bf16[1,2,64,640]{3,2,1,0:T(8,128)(2,1)}, bf16[1,2560,640]{2,1,0:T(8,128)(2,1)}, ...), branch_computations={%region_5.5_spmd, %region_6.8_spmd} | conditional | flops 1720939136 | bytes 34157632 | solution.py:158
  209.0 21.8 %reduce-scatter.6.cloned.1.call-done = bf16[640,128]{1,0:T(8,128)(2,1)} async-done(((bf16[2560,128]{1,0:T(8,128)(2,1)}), bf16[640,128]{1,0:T(8,128)(2,1)}) %reduce-scatter.6.cloned.1.call-update) | async-done | bytes 163856 | tf_op jit(solution)/shard_map/while
  254.7 12.0 %psum.23 = bf16[128,128]{1,0:T(8,128)(2,1)S(1)} all-reduce(f32[128,128]{1,0:T(8,128)S(1)} %get-tuple-element.638), channel_id=1, replica_groups=mesh['section'=4,'dp'=2,'tensor'=4] {'tensor'}, use_global_device_ids=true, to_apply=%region_4.4 | all-reduce | flops 16384 | bytes 98304 | tf_op jit(solution)/shard_map/while/body/eval_jaxpr/psum | solution.py:151
  267.6 22.1 %conditional.5 = (bf16[128,2560]{1,0:T(8,128)(2,1)S(1)}) conditional(s32[]{:T(128)} %convert_element_type.120, () %tuple.63, (bf16[1,2560,640]{2,1,0:T(8,128)(2,1)}, bf16[128,2560]{1,0:T(8,128)(2,1)}, bf16[128,128]{1,0:T(8,128)(2,1)S(1)}, bf16[1,2,64,640]{3,2,1,0:T(8,128)(2,1)}, bf16[1,2560,640]{2,1,0:T(8,128)(2,1)}, ...), branch_computations={%region_5.5_spmd, %region_6.8_spmd} | conditional | flops 1720939136 | bytes 34157632 | solution.py:158
  290.8 22.7 %reduce-scatter.6.cloned.1.call-done = bf16[640,128]{1,0:T(8,128)(2,1)} async-done(((bf16[2560,128]{1,0:T(8,128)(2,1)}), bf16[640,128]{1,0:T(8,128)(2,1)}) %reduce-scatter.6.cloned.1.call-update) | async-done | bytes 163856 | tf_op jit(solution)/shard_map/while
  337.4 12.0 %psum.23 = bf16[128,128]{1,0:T(8,128)(2,1)S(1)} all-reduce(f32[128,128]{1,0:T(8,128)S(1)} %get-tuple-element.638), channel_id=1, replica_groups=mesh['section'=4,'dp'=2,'tensor'=4] {'tensor'}, use_global_device_ids=true, to_apply=%region_4.4 | all-reduce | flops 16384 | bytes 98304 | tf_op jit(solution)/shard_map/while/body/eval_jaxpr/psum | solution.py:151
  350.3 22.1 %conditional.5 = (bf16[128,2560]{1,0:T(8,128)(2,1)S(1)}) conditional(s32[]{:T(128)} %convert_element_type.120, () %tuple.63, (bf16[1,2560,640]{2,1,0:T(8,128)(2,1)}, bf16[128,2560]{1,0:T(8,128)(2,1)}, bf16[128,128]{1,0:T(8,128)(2,1)S(1)}, bf16[1,2,64,640]{3,2,1,0:T(8,128)(2,1)}, bf16[1,2560,640]{2,1,0:T(8,128)(2,1)}, ...), branch_computations={%region_5.5_spmd, %region_6.8_spmd} | conditional | flops 1720939136 | bytes 34157632 | solution.py:158
  373.5 23.6 %reduce-scatter.6.cloned.1.call-done = bf16[640,128]{1,0:T(8,128)(2,1)} async-done(((bf16[2560,128]{1,0:T(8,128)(2,1)}), bf16[640,128]{1,0:T(8,128)(2,1)}) %reduce-scatter.6.cloned.1.call-update) | async-done | bytes 163856 | tf_op jit(solution)/shard_map/while
  419.3 12.0 %psum.23 = bf16[128,128]{1,0:T(8,128)(2,1)S(1)} all-reduce(f32[128,128]{1,0:T(8,128)S(1)} %get-tuple-element.638), channel_id=1, replica_groups=mesh['section'=4,'dp'=2,'tensor'=4] {'tensor'}, use_global_device_ids=true, to_apply=%region_4.4 | all-reduce | flops 16384 | bytes 98304 | tf_op jit(solution)/shard_map/while/body/eval_jaxpr/psum | solution.py:151
  433.5 47.2 %reduce-scatter.6.cloned.1.call-done = bf16[640,128]{1,0:T(8,128)(2,1)} async-done(((bf16[2560,128]{1,0:T(8,128)(2,1)}), bf16[640,128]{1,0:T(8,128)(2,1)}) %reduce-scatter.6.cloned.1.call-update) | async-done | bytes 163856 | tf_op jit(solution)/shard_map/while
  502.9 12.0 %psum.23 = bf16[128,128]{1,0:T(8,128)(2,1)S(1)} all-reduce(f32[128,128]{1,0:T(8,128)S(1)} %get-tuple-element.638), channel_id=1, replica_groups=mesh['section'=4,'dp'=2,'tensor'=4] {'tensor'}, use_global_device_ids=true, to_apply=%region_4.4 | all-reduce | flops 16384 | bytes 98304 | tf_op jit(solution)/shard_map/while/body/eval_jaxpr/psum | solution.py:151
  517.1 47.2 %reduce-scatter.6.cloned.1.call-done = bf16[640,128]{1,0:T(8,128)(2,1)} async-done(((bf16[2560,128]{1,0:T(8,128)(2,1)}), bf16[640,128]{1,0:T(8,128)(2,1)}) %reduce-scatter.6.cloned.1.call-update) | async-done | bytes 163856 | tf_op jit(solution)/shard_map/while
  586.5 12.0 %psum.23 = bf16[128,128]{1,0:T(8,128)(2,1)S(1)} all-reduce(f32[128,128]{1,0:T(8,128)S(1)} %get-tuple-element.638), channel_id=1, replica_groups=mesh['section'=4,'dp'=2,'tensor'=4] {'tensor'}, use_global_device_ids=true, to_apply=%region_4.4 | all-reduce | flops 16384 | bytes 98304 | tf_op jit(solution)/shard_map/while/body/eval_jaxpr/psum | solution.py:151
  600.7 47.2 %reduce-scatter.6.cloned.1.call-done = bf16[640,128]{1,0:T(8,128)(2,1)} async-done(((bf16[2560,128]{1,0:T(8,128)(2,1)}), bf16[640,128]{1,0:T(8,128)(2,1)}) %reduce-scatter.6.cloned.1.call-update) | async-done | bytes 163856 | tf_op jit(solution)/shard_map/while
  658.3 43.7 %all-reduce.2.cloned.1.call-done = bf16[4,128,640]{2,1,0:T(8,128)(2,1)} async-done(((bf16[4,128,640]{2,1,0:T(8,128)(2,1)}), bf16[4,128,640]{2,1,0:T(8,128)(2,1)}) %all-reduce.2.cloned.1.call-update) | async-done | bytes 655376 | tf_op jit(solution)/shard_map/psum | solution.py:20
  702.0 26.7 %all-gather.5.cloned.1.call-done = bf16[4,128,2560]{2,1,0:T(8,128)(2,1)} async-done(((bf16[4,128,640]{2,1,0:T(8,128)(2,1)}), bf16[4,128,2560]{2,1,0:T(8,128)(2,1)}) %all-gather.5.cloned.1.call-update) | async-done | bytes 2621456 | tf_op jit(solution)/shard_map/all_gather | solution.py:207
  (238 shorter events, 249.9 us)
Async XLA Ops:
  6.5 61.6 %all-gather.3.cloned.1.call-start = ((), (), s32[]{:S(2)}) async-start(), calls=%async_computation.1 | async-start | bytes 5570560 | tf_op jit(solution)/shard_map/all_gather | solution.py:124
  9.2 68.3 %copy-start.1 = (f32[1,2560]{1,0:T(1,128)S(1)}, f32[1,2560]{1,0:T(1,128)}, u32[]{:S(2)}) copy-start(f32[1,2560]{1,0:T(1,128)} %param.19) | copy-start | bytes 30724
  9.2 68.3 %copy-start.2 = (s32[4]{0:T(128)S(1)}, s32[4]{0:T(128)}, u32[]{:S(2)}) copy-start(s32[4]{0:T(128)} %param.18) | copy-start | bytes 52
  77.5 71.5 %reduce-scatter.6.cloned.1.call-start = ((), (), s32[]{:S(2)}) async-start(), calls=%async_computation.4 | async-start | bytes 819200 | tf_op jit(solution)/shard_map/while
  109.7 9.8 %copy-start = (bf16[1,2560,640]{2,1,0:T(8,128)(2,1)S(1)}, bf16[1,2560,640]{2,1,0:T(8,128)(2,1)}, u32[]{:S(2)}) copy-start(bf16[1,2560,640]{2,1,0:T(8,128)(2,1)} %get-tuple-element.398) | copy-start | bytes 9830404 | tf_op jit(solution)/shard_map/while/body/eval_jaxpr/cond
  118.2 1.3 copy-start.3
  151.7 6.6 collective-permute-start
  158.3 72.4 %reduce-scatter.6.cloned.1.call-start = ((), (), s32[]{:S(2)}) async-start(), calls=%async_computation.4 | async-start | bytes 819200 | tf_op jit(solution)/shard_map/while
  190.3 9.8 %copy-start = (bf16[1,2560,640]{2,1,0:T(8,128)(2,1)S(1)}, bf16[1,2560,640]{2,1,0:T(8,128)(2,1)}, u32[]{:S(2)}) copy-start(bf16[1,2560,640]{2,1,0:T(8,128)(2,1)} %get-tuple-element.398) | copy-start | bytes 9830404 | tf_op jit(solution)/shard_map/while/body/eval_jaxpr/cond
  233.5 6.7 collective-permute-start
  240.2 73.3 %reduce-scatter.6.cloned.1.call-start = ((), (), s32[]{:S(2)}) async-start(), calls=%async_computation.4 | async-start | bytes 819200 | tf_op jit(solution)/shard_map/while
  272.2 9.8 %copy-start = (bf16[1,2560,640]{2,1,0:T(8,128)(2,1)S(1)}, bf16[1,2560,640]{2,1,0:T(8,128)(2,1)}, u32[]{:S(2)}) copy-start(bf16[1,2560,640]{2,1,0:T(8,128)(2,1)} %get-tuple-element.398) | copy-start | bytes 9830404 | tf_op jit(solution)/shard_map/while/body/eval_jaxpr/cond
  316.2 6.6 collective-permute-start
  322.9 74.2 %reduce-scatter.6.cloned.1.call-start = ((), (), s32[]{:S(2)}) async-start(), calls=%async_computation.4 | async-start | bytes 819200 | tf_op jit(solution)/shard_map/while
  354.9 9.8 %copy-start = (bf16[1,2560,640]{2,1,0:T(8,128)(2,1)S(1)}, bf16[1,2560,640]{2,1,0:T(8,128)(2,1)}, u32[]{:S(2)}) copy-start(bf16[1,2560,640]{2,1,0:T(8,128)(2,1)} %get-tuple-element.398) | copy-start | bytes 9830404 | tf_op jit(solution)/shard_map/while/body/eval_jaxpr/cond
  399.8 6.7 collective-permute-start
  406.4 74.2 %reduce-scatter.6.cloned.1.call-start = ((), (), s32[]{:S(2)}) async-start(), calls=%async_computation.4 | async-start | bytes 819200 | tf_op jit(solution)/shard_map/while
  483.4 6.7 collective-permute-start
  490.1 74.2 %reduce-scatter.6.cloned.1.call-start = ((), (), s32[]{:S(2)}) async-start(), calls=%async_computation.4 | async-start | bytes 819200 | tf_op jit(solution)/shard_map/while
  567.0 6.6 collective-permute-start
  573.7 74.2 %reduce-scatter.6.cloned.1.call-start = ((), (), s32[]{:S(2)}) async-start(), calls=%async_computation.4 | async-start | bytes 819200 | tf_op jit(solution)/shard_map/while
  650.6 6.7 collective-permute-start
  657.3 44.7 %all-reduce.2.cloned.1.call-start = ((), (), s32[]{:S(2)}) async-start(), calls=%async_computation.2 | async-start | bytes 1310720 | tf_op jit(solution)/shard_map/psum | solution.py:20
  658.2 70.5 %all-gather.5.cloned.1.call-start = ((), (), s32[]{:S(2)}) async-start(), calls=%async_computation.3 | async-start | bytes 3276800 | tf_op jit(solution)/shard_map/all_gather | solution.py:207
  (3 other events, 3.8 us)
Sparse Core Ops, SparseCore 0:
  9.6 58.4 all-gather.2
  128.4 20.5 reduce-scatter.5
  209.1 21.6 reduce-scatter.5
  290.9 22.5 reduce-scatter.5
  373.6 23.4 reduce-scatter.5
  433.6 47.0 reduce-scatter.5
  517.2 47.0 reduce-scatter.5
  600.8 47.0 reduce-scatter.5
  660.4 41.5 all-reduce.1
  703.4 25.2 all-gather.4
where the time goes:
time: 740 us; the launch traced here: 737 us
  waiting for transfers between devices  383 us (52%)
  blocking collectives  133 us (18%)
  matrix products  72 us (10%)
  local copies, waits for them, and re-layouts  65.6 us (9%)
  loops' own time  27.8 us (4%)
  starting transfers between devices  23.8 us (3%)
  other arithmetic  19.2 us (3%)
  between operations  13.5 us (2%)
    while x14, waiting for transfers between devices  231 us
    psum x7, blocking collectives, compute(): summed_codes = lax.psum(part_codes, 'tensor')  83.2 us
    all_gather x1, waiting for transfers between devices, shards(): entire = lax.all_gather(inputs, ('section', 'tensor'), axis=3, tiled=True)  58.9 us
    all_gather x7, blocking collectives, advance(): complete_result = lax.all_gather(owned, 'tensor', axis=1, tiled=True)  49.7 us
    psum x1, waiting for transfers between devices, spread(): return lax.psum(jnp.where(mine, array, jnp.zeros_like(array)), axis)  43.7 us
    another operation x1, loops' own time, shards(): arrived, stored = lax.fori_loop(0, step_count, advance, (initial, stored))  27.4 us
    all_gather x1, waiting for transfers between devices, shards(): complete = lax.all_gather(result, 'tensor', axis=2, tiled=True)  26.7 us
    ppermute x7, starting transfers between devices, shifted(): lax.ppermute(value, axis, [(source, source + steps) for source in range(l...  23.7 us
  transfers between devices with their start and end apart: 17, of which 17 were waited for; matrix products, arithmetic and copies ran while one was open for 0% of the time, Pallas kernels for 0%

commit v1 on v0

--- a/solution.py
+++ b/solution.py
@@ -148,7 +148,8 @@
                 jnp.zeros((tok_rows, lowrank_width), jnp.float32),
             ),
         )
-        summed_codes = lax.psum(part_codes, "tensor")
+        pieces = lax.all_gather(part_codes, "tensor", axis=0, tiled=False)
+        summed_codes = pieces.sum(axis=0)
         column_job = (
             lax.broadcasted_iota(jnp.int32, (lowrank_width,), 0) // ADAPTER_RANK % ADAPTER_JOBS
         )

time: 740 us -> 702 us (0.949)
  blocking collectives: 133 us -> 90.5 us
    psum x7 -> x0, blocking collectives: 83.2 us -> none  [compute(): summed_codes = lax.psum(part_codes, 'tensor')]
    all_gather x0 -> x7, blocking collectives: none -> 40.9 us  [compute(): pieces = lax.all_gather(part_codes, 'tensor', axis=0, tiled=False)]
where the time goes in v1:
time: 702 us; the launch traced here: 699 us
  waiting for transfers between devices  387 us (55%)
  blocking collectives  90.5 us (13%)
  matrix products  72 us (10%)
  local copies, waits for them, and re-layouts  65.6 us (9%)
  loops' own time  27.8 us (4%)
  starting transfers between devices  23.8 us (3%)
  other arithmetic  19.3 us (3%)
  between operations  13.5 us (2%)
    while x14, waiting for transfers between devices  235 us
    all_gather x1, waiting for transfers between devices, shards(): entire = lax.all_gather(inputs, ('section', 'tensor'), axis=3, tiled=True)  58.9 us
    all_gather x7, blocking collectives, advance(): complete_result = lax.all_gather(owned, 'tensor', axis=1, tiled=True)  49.6 us
    psum x1, waiting for transfers between devices, spread(): return lax.psum(jnp.where(mine, array, jnp.zeros_like(array)), axis)  43.7 us
    all_gather x7, blocking collectives, compute(): pieces = lax.all_gather(part_codes, 'tensor', axis=0, tiled=False)  40.9 us
    another operation x1, loops' own time, shards(): arrived, stored = lax.fori_loop(0, step_count, advance, (initial, stored))  27.4 us
    all_gather x1, waiting for transfers between devices, shards(): complete = lax.all_gather(result, 'tensor', axis=2, tiled=True)  26.5 us
    ppermute x7, starting transfers between devices, shifted(): lax.ppermute(value, axis, [(source, source + steps) for source in range(l...  23.7 us
  transfers between devices with their start and end apart: 17, of which 17 were waited for; matrix products, arithmetic and copies ran while one was open for 0% of the time, Pallas kernels for 0%

profile of v1, /device:TPU:0, one launch (start us, length us, event | category | flops | bytes accessed | tf_op | source)
XLA Modules:
  0.0 699.3 jit_solution(8982303179844730280)
XLA Ops:
  9.2 58.9 %all-gather.6.cloned.1.call-done = bf16[4,2,64,2560]{2,0,1,3:T(4,128)(2,1)} async-done(((bf16[4,2,64,160]{2,0,1,3:T(4,128)(2,1)}), bf16[4,2,64,2560]{2,0,1,3:T(4,128)(2,1)}) %all-gather.6.cloned.1.call-update) | async-done | bytes 2621456 | tf_op jit(solution)/shard_map/all_gather | solution.py:124
  68.1 8.5 %copy.28 = bf16[4,2,64,2560]{3,2,1,0:T(8,128)(2,1)} copy(bf16[4,2,64,2560]{2,0,1,3:T(4,128)(2,1)} %all-gather.6.cloned.1.call-done) | data formatting | bytes 5242880 | tf_op jit(solution)/shard_map/while | solution.py:206
  77.5 541.9 %while.17 = (s32[]{:T(128)}, bf16[128,640]{1,0:T(8,128)(2,1)S(1)}, bf16[4,128,640]{2,1,0:T(8,128)(2,1)}, pred[]{:T(512)}, s32[4]{0:T(128)S(1)}, /*index=5*/bf16[...) while((s32[]{:T(128)}, bf16[128,640]{1,0:T(8,128)(2,1)S(1)}, ...), condition=%wide.region_10.11_spmd, body=%wide.region_0.10_spmd.sunk | while | flops 1744780416 | bytes 45433628 | solution.py:206
  82.6 7.9 %all_gather.39 = bf16[128,2560]{1,0:T(8,128)(2,1)S(1)} all-gather(bf16[128,640]{1,0:T(8,128)(2,1)S(1)} %dynamic-slice_select_fusion.2), channel_id=1, replica_groups=mesh['section'=4,'dp'=2,'tensor'=4] {'tensor'}, dimensions={1}, use_global_device_ids=true | all-gather | bytes 819200 | tf_op jit(solution)/shard_map/while/body/eval_jaxpr/all_gather | solution.py:195
  93.0 5.9 all-gather.2
  99.8 22.1 %conditional.5 = (bf16[128,2560]{1,0:T(8,128)(2,1)S(1)}) conditional(s32[]{:T(128)} %convert_element_type.120, () %tuple.63, (bf16[1,2560,640]{2,1,0:T(8,128)(2,1)}, bf16[128,2560]{1,0:T(8,128)(2,1)}, bf16[128,128]{1,0:T(8,128)(2,1)S(1)}, bf16[1,2,64,640]{3,2,1,0:T(8,128)(2,1)}, bf16[1,2560,640]{2,1,0:T(8,128)(2,1)}, ...), branch_computations={%region_5.5_spmd, %region_6.8_spmd} | conditional | flops 1720939136 | bytes 34157632 | solution.py:159
  123.0 19.8 %reduce-scatter.6.cloned.1.call-done = bf16[640,128]{1,0:T(8,128)(2,1)} async-done(((bf16[2560,128]{1,0:T(8,128)(2,1)}), bf16[640,128]{1,0:T(8,128)(2,1)}) %reduce-scatter.6.cloned.1.call-update) | async-done | bytes 163856 | tf_op jit(solution)/shard_map/while
  157.2 7.0 all_gather.39
  173.5 22.1 %conditional.5 = (bf16[128,2560]{1,0:T(8,128)(2,1)S(1)}) conditional(s32[]{:T(128)} %convert_element_type.120, () %tuple.63, (bf16[1,2560,640]{2,1,0:T(8,128)(2,1)}, bf16[128,2560]{1,0:T(8,128)(2,1)}, bf16[128,128]{1,0:T(8,128)(2,1)S(1)}, bf16[1,2,64,640]{3,2,1,0:T(8,128)(2,1)}, bf16[1,2560,640]{2,1,0:T(8,128)(2,1)}, ...), branch_computations={%region_5.5_spmd, %region_6.8_spmd} | conditional | flops 1720939136 | bytes 34157632 | solution.py:159
  196.7 22.6 %reduce-scatter.6.cloned.1.call-done = bf16[640,128]{1,0:T(8,128)(2,1)} async-done(((bf16[2560,128]{1,0:T(8,128)(2,1)}), bf16[640,128]{1,0:T(8,128)(2,1)}) %reduce-scatter.6.cloned.1.call-update) | async-done | bytes 163856 | tf_op jit(solution)/shard_map/while
  233.7 6.9 all_gather.39
  250.0 22.1 %conditional.5 = (bf16[128,2560]{1,0:T(8,128)(2,1)S(1)}) conditional(s32[]{:T(128)} %convert_element_type.120, () %tuple.63, (bf16[1,2560,640]{2,1,0:T(8,128)(2,1)}, bf16[128,2560]{1,0:T(8,128)(2,1)}, bf16[128,128]{1,0:T(8,128)(2,1)S(1)}, bf16[1,2,64,640]{3,2,1,0:T(8,128)(2,1)}, bf16[1,2560,640]{2,1,0:T(8,128)(2,1)}, ...), branch_computations={%region_5.5_spmd, %region_6.8_spmd} | conditional | flops 1720939136 | bytes 34157632 | solution.py:159
  273.2 23.6 %reduce-scatter.6.cloned.1.call-done = bf16[640,128]{1,0:T(8,128)(2,1)} async-done(((bf16[2560,128]{1,0:T(8,128)(2,1)}), bf16[640,128]{1,0:T(8,128)(2,1)}) %reduce-scatter.6.cloned.1.call-update) | async-done | bytes 163856 | tf_op jit(solution)/shard_map/while
  311.1 7.0 all_gather.39
  327.4 22.1 %conditional.5 = (bf16[128,2560]{1,0:T(8,128)(2,1)S(1)}) conditional(s32[]{:T(128)} %convert_element_type.120, () %tuple.63, (bf16[1,2560,640]{2,1,0:T(8,128)(2,1)}, bf16[128,2560]{1,0:T(8,128)(2,1)}, bf16[128,128]{1,0:T(8,128)(2,1)S(1)}, bf16[1,2,64,640]{3,2,1,0:T(8,128)(2,1)}, bf16[1,2560,640]{2,1,0:T(8,128)(2,1)}, ...), branch_computations={%region_5.5_spmd, %region_6.8_spmd} | conditional | flops 1720939136 | bytes 34157632 | solution.py:159
  350.6 24.5 %reduce-scatter.6.cloned.1.call-done = bf16[640,128]{1,0:T(8,128)(2,1)} async-done(((bf16[2560,128]{1,0:T(8,128)(2,1)}), bf16[640,128]{1,0:T(8,128)(2,1)}) %reduce-scatter.6.cloned.1.call-update) | async-done | bytes 163856 | tf_op jit(solution)/shard_map/while
  389.4 7.0 all_gather.39
  405.3 48.1 %reduce-scatter.6.cloned.1.call-done = bf16[640,128]{1,0:T(8,128)(2,1)} async-done(((bf16[2560,128]{1,0:T(8,128)(2,1)}), bf16[640,128]{1,0:T(8,128)(2,1)}) %reduce-scatter.6.cloned.1.call-update) | async-done | bytes 163856 | tf_op jit(solution)/shard_map/while
  467.8 6.9 all_gather.39
  483.6 48.1 %reduce-scatter.6.cloned.1.call-done = bf16[640,128]{1,0:T(8,128)(2,1)} async-done(((bf16[2560,128]{1,0:T(8,128)(2,1)}), bf16[640,128]{1,0:T(8,128)(2,1)}) %reduce-scatter.6.cloned.1.call-update) | async-done | bytes 163856 | tf_op jit(solution)/shard_map/while
  546.1 6.9 all_gather.39
  561.9 48.1 %reduce-scatter.6.cloned.1.call-done = bf16[640,128]{1,0:T(8,128)(2,1)} async-done(((bf16[2560,128]{1,0:T(8,128)(2,1)}), bf16[640,128]{1,0:T(8,128)(2,1)}) %reduce-scatter.6.cloned.1.call-update) | async-done | bytes 163856 | tf_op jit(solution)/shard_map/while
  620.4 43.7 %all-reduce.2.cloned.1.call-done = bf16[4,128,640]{2,1,0:T(8,128)(2,1)} async-done(((bf16[4,128,640]{2,1,0:T(8,128)(2,1)}), bf16[4,128,640]{2,1,0:T(8,128)(2,1)}) %all-reduce.2.cloned.1.call-update) | async-done | bytes 655376 | tf_op jit(solution)/shard_map/psum | solution.py:20
  664.1 26.5 %all-gather.8.cloned.1.call-done = bf16[4,128,2560]{2,1,0:T(8,128)(2,1)} async-done(((bf16[4,128,640]{2,1,0:T(8,128)(2,1)}), bf16[4,128,2560]{2,1,0:T(8,128)(2,1)}) %all-gather.8.cloned.1.call-update) | async-done | bytes 2621456 | tf_op jit(solution)/shard_map/all_gather | solution.py:208
  (245 shorter events, 243.3 us)
Async XLA Ops:
  6.5 61.6 %all-gather.6.cloned.1.call-start = ((), (), s32[]{:S(2)}) async-start(), calls=%async_computation.1 | async-start | bytes 5570560 | tf_op jit(solution)/shard_map/all_gather | solution.py:124
  9.2 68.3 %copy-start.1 = (f32[1,2560]{1,0:T(1,128)S(1)}, f32[1,2560]{1,0:T(1,128)}, u32[]{:S(2)}) copy-start(f32[1,2560]{1,0:T(1,128)} %param.19) | copy-start | bytes 30724
  9.2 68.3 %copy-start.2 = (s32[4]{0:T(128)S(1)}, s32[4]{0:T(128)}, u32[]{:S(2)}) copy-start(s32[4]{0:T(128)} %param.18) | copy-start | bytes 52
  77.5 65.3 %reduce-scatter.6.cloned.1.call-start = ((), (), s32[]{:S(2)}) async-start(), calls=%async_computation.4 | async-start | bytes 819200 | tf_op jit(solution)/shard_map/while
  104.4 9.8 %copy-start = (bf16[1,2560,640]{2,1,0:T(8,128)(2,1)S(1)}, bf16[1,2560,640]{2,1,0:T(8,128)(2,1)}, u32[]{:S(2)}) copy-start(bf16[1,2560,640]{2,1,0:T(8,128)(2,1)} %get-tuple-element.398) | copy-start | bytes 9830404 | tf_op jit(solution)/shard_map/while/body/eval_jaxpr/cond
  113.0 1.3 copy-start.3
  145.5 6.6 collective-permute-start
  152.2 67.1 %reduce-scatter.6.cloned.1.call-start = ((), (), s32[]{:S(2)}) async-start(), calls=%async_computation.4 | async-start | bytes 819200 | tf_op jit(solution)/shard_map/while
  178.0 9.8 %copy-start = (bf16[1,2560,640]{2,1,0:T(8,128)(2,1)S(1)}, bf16[1,2560,640]{2,1,0:T(8,128)(2,1)}, u32[]{:S(2)}) copy-start(bf16[1,2560,640]{2,1,0:T(8,128)(2,1)} %get-tuple-element.398) | copy-start | bytes 9830404 | tf_op jit(solution)/shard_map/while/body/eval_jaxpr/cond
  222.0 6.7 collective-permute-start
  228.7 68.0 %reduce-scatter.6.cloned.1.call-start = ((), (), s32[]{:S(2)}) async-start(), calls=%async_computation.4 | async-start | bytes 819200 | tf_op jit(solution)/shard_map/while
  254.5 9.8 %copy-start = (bf16[1,2560,640]{2,1,0:T(8,128)(2,1)S(1)}, bf16[1,2560,640]{2,1,0:T(8,128)(2,1)}, u32[]{:S(2)}) copy-start(bf16[1,2560,640]{2,1,0:T(8,128)(2,1)} %get-tuple-element.398) | copy-start | bytes 9830404 | tf_op jit(solution)/shard_map/while/body/eval_jaxpr/cond
  299.4 6.6 collective-permute-start
  306.1 69.0 %reduce-scatter.6.cloned.1.call-start = ((), (), s32[]{:S(2)}) async-start(), calls=%async_computation.4 | async-start | bytes 819200 | tf_op jit(solution)/shard_map/while
  332.0 9.8 %copy-start = (bf16[1,2560,640]{2,1,0:T(8,128)(2,1)S(1)}, bf16[1,2560,640]{2,1,0:T(8,128)(2,1)}, u32[]{:S(2)}) copy-start(bf16[1,2560,640]{2,1,0:T(8,128)(2,1)} %get-tuple-element.398) | copy-start | bytes 9830404 | tf_op jit(solution)/shard_map/while/body/eval_jaxpr/cond
  377.7 6.7 collective-permute-start
  384.4 68.9 %reduce-scatter.6.cloned.1.call-start = ((), (), s32[]{:S(2)}) async-start(), calls=%async_computation.4 | async-start | bytes 819200 | tf_op jit(solution)/shard_map/while
  456.1 6.7 collective-permute-start
  462.7 69.0 %reduce-scatter.6.cloned.1.call-start = ((), (), s32[]{:S(2)}) async-start(), calls=%async_computation.4 | async-start | bytes 819200 | tf_op jit(solution)/shard_map/while
  534.4 6.7 collective-permute-start
  541.1 68.9 %reduce-scatter.6.cloned.1.call-start = ((), (), s32[]{:S(2)}) async-start(), calls=%async_computation.4 | async-start | bytes 819200 | tf_op jit(solution)/shard_map/while
  612.7 6.7 collective-permute-start
  619.4 44.7 %all-reduce.2.cloned.1.call-start = ((), (), s32[]{:S(2)}) async-start(), calls=%async_computation.2 | async-start | bytes 1310720 | tf_op jit(solution)/shard_map/psum | solution.py:20
  620.4 70.3 %all-gather.8.cloned.1.call-start = ((), (), s32[]{:S(2)}) async-start(), calls=%async_computation.3 | async-start | bytes 3276800 | tf_op jit(solution)/shard_map/all_gather | solution.py:208
  (3 other events, 3.8 us)
Sparse Core Ops, SparseCore 0:
  9.6 58.4 all-gather.5
  123.1 19.6 reduce-scatter.5
  196.8 22.4 reduce-scatter.5
  273.3 23.4 reduce-scatter.5
  350.7 24.2 reduce-scatter.5
  405.4 47.9 reduce-scatter.5
  483.7 47.9 reduce-scatter.5
  562.0 47.9 reduce-scatter.5
  622.6 41.5 all-reduce.1
  665.5 25.0 all-gather.7
